TPU v7x, 32 devices: a whole 2x2x4 slice. The times are simulated.
32 devices in a mesh: shard: 4 (over y, x), ctx: 2 (over core), tp: 4 (over z).
Axes of the slice: x: 2, y: 2, z: 4, core: 2. Of those that a mesh axis runs over, the one named last changes fastest.
Arguments:
- tokens: bfloat16 [4, 2048, 2048], P('shard', 'ctx'), may hold values from -6 to 6
- lengths: int32 [4], P('shard'), may hold values from 512 to 2048, as said below
- cotangent: bfloat16 [4, 2048, 2048], P('shard', 'ctx'), may hold values from -6 to 6
- w_query: float32 [2048, 2048], P(('shard', 'ctx'), 'tp'), may hold values from -0.1875 to 0.1875
- w_key: float32 [2048, 2048], P(('shard', 'ctx'), 'tp'), may hold values from -0.1875 to 0.1875
- w_value: float32 [2048, 2048], P(('shard', 'ctx'), 'tp'), may hold values from -0.125 to 0.125
- w_output: float32 [2048, 2048], P('tp', ('shard', 'ctx')), may hold values from -1 to 1
- w_gate: float32 [2048, 8192], P(('shard', 'ctx'), 'tp'), may hold values from -0.125 to 0.125
- w_up: float32 [2048, 8192], P(('shard', 'ctx'), 'tp'), may hold values from -0.125 to 0.125
- w_down: float32 [8192, 2048], P('tp', ('shard', 'ctx')), may hold values from -0.0625 to 0.0625
Outputs:
- output: bfloat16 [4, 2048, 2048], P('shard', 'ctx')
- grad_tokens: float32 [4, 2048, 2048], P('shard', 'ctx')
- grad_query: float32 [2048, 2048], P(('shard', 'ctx'), 'tp')
- grad_key: float32 [2048, 2048], P(('shard', 'ctx'), 'tp')
- grad_value: float32 [2048, 2048], P(('shard', 'ctx'), 'tp')
- grad_output: float32 [2048, 2048], P('tp', ('shard', 'ctx'))
- grad_gate: float32 [2048, 8192], P(('shard', 'ctx'), 'tp')
- grad_up: float32 [2048, 8192], P(('shard', 'ctx'), 'tp')
- grad_down: float32 [8192, 2048], P('tp', ('shard', 'ctx'))
Inputs may be any that keep to these rules, and one draw needn't show every extreme that they name: Slots 0 to lengths[b] - 1 of sequence b are valid, the rest padding; some sequence is full and some has 512 valid slots.
All inputs are finite; a program needn't handle non-finite values.
Results may differ from a plain program's by a relative error of at most 0.014.
The roundings to bfloat16 on the way count: a program that leaves them out, or rounds other values in their place, can miss the bound.
Values may be sent and summed in bfloat16 or wider, within the bound.
A program may use at most 256 MiB of HBM per device.

v0:
```python
import jax
import jax.numpy as jnp
from jax import lax
from jax.sharding import PartitionSpec as P

HEAD_DIM = 128
EPSILON = 1e-05


def normalize(values):
    center = values - jnp.mean(values, axis=-1, keepdims=True)
    inv_scale = lax.rsqrt(jnp.mean(center * center, axis=-1, keepdims=True) + EPSILON)
    return (center * inv_scale, inv_scale)


def norm_back(normed, inv_scale, upstream):
    first_mean = jnp.mean(upstream, axis=-1, keepdims=True)
    second_mean = jnp.mean(upstream * normed, axis=-1, keepdims=True)
    return inv_scale * (upstream - first_mean - normed * second_mean)


def rope_tables(row_count, head_size, offset):
    positions = (jnp.arange(row_count) + offset).astype(jnp.float32)
    inverse = 10000.0 ** (-(jnp.arange(head_size // 2).astype(jnp.float32) * 2.0) / head_size)
    angles = positions[:, None] * inverse[None, :]
    angles = jnp.concatenate([angles, angles], axis=-1)
    return (jnp.cos(angles)[:, None, :], jnp.sin(angles)[:, None, :])


def turn_half(values):
    half_dim = values.shape[-1] // 2
    return jnp.concatenate([-values[..., half_dim:], values[..., :half_dim]], axis=-1)


def rotate(values, cosine, sine_table):
    return values * cosine + turn_half(values) * sine_table


def rotate_back(values, cosine, sine_table):
    return values * cosine - turn_half(values) * sine_table


def score_block(query_rows, keys_seq, length, row_start):
    block_rows = query_rows.shape[0]
    key_pos = jnp.arange(keys_seq.shape[0])
    row_pos = row_start + jnp.arange(block_rows)
    scores = jnp.einsum(
        "qhd,khd->hqk", query_rows, keys_seq, preferred_element_type=jnp.float32
    ) * HEAD_DIM ** (-0.5)
    allowed = (key_pos[None, :] <= row_pos[:, None]) & (key_pos[None, :] < length)
    return jnp.where(allowed[None], scores, -1e30)


def attend_forward(queries_seq, keys_seq, values_seq, length, offset):
    half_len, head_count, head_size = queries_seq.shape
    block_rows = min(512, half_len)
    block_count = half_len // block_rows
    grouped = queries_seq.reshape(block_count, block_rows, head_count, head_size)

    def one_block(paired):
        query_rows, block_index = paired
        scores = score_block(query_rows, keys_seq, length, offset + block_index * block_rows)
        row_peak = jnp.max(scores, axis=-1, keepdims=True)
        log_total = jnp.log(jnp.sum(jnp.exp(scores - row_peak), axis=-1, keepdims=True)) + row_peak
        probability = jnp.exp(scores - log_total).astype(jnp.bfloat16)
        attended = jnp.einsum(
            "hqk,khd->qhd", probability, values_seq, preferred_element_type=jnp.float32
        )
        return (attended.astype(jnp.bfloat16), log_total[..., 0])

    attended, log_totals = lax.map(one_block, (grouped, jnp.arange(block_count)))
    return (attended.reshape(half_len, head_count, head_size), log_totals)


def attend_backward(queries_seq, keys_seq, values_seq, length, offset, log_totals, grad_seq):
    half_len, head_count, head_size = queries_seq.shape
    block_rows = min(512, half_len)
    block_count = half_len // block_rows
    score_scale = HEAD_DIM ** (-0.5)
    grouped = queries_seq.reshape(block_count, block_rows, head_count, head_size)
    grad_grouped = grad_seq.reshape(block_count, block_rows, head_count, head_size)

    def one_block(carried, paired):
        query_rows, grad_rows, log_rows, block_index = paired
        scores = score_block(query_rows, keys_seq, length, offset + block_index * block_rows)
        probability = jnp.exp(scores - log_rows[..., None])
        prob_low = probability.astype(jnp.bfloat16)
        grad_prob = jnp.einsum(
            "qhd,khd->hqk", grad_rows, values_seq, preferred_element_type=jnp.float32
        )
        inner_sum = jnp.sum(probability * grad_prob, axis=-1, keepdims=True)
        grad_scores = (probability * (grad_prob - inner_sum)).astype(jnp.bfloat16)
        grad_query_rows = (
            jnp.einsum("hqk,khd->qhd", grad_scores, keys_seq, preferred_element_type=jnp.float32)
            * score_scale
        )
        key_part = (
            jnp.einsum("hqk,qhd->khd", grad_scores, query_rows, preferred_element_type=jnp.float32)
            * score_scale
        )
        value_part = jnp.einsum(
            "hqk,qhd->khd", prob_low, grad_rows, preferred_element_type=jnp.float32
        )
        return ((carried[0] + key_part, carried[1] + value_part), grad_query_rows)

    empty = jnp.zeros(keys_seq.shape, jnp.float32)
    sums, grad_queries = lax.scan(
        one_block, (empty, empty), (grouped, grad_grouped, log_totals, jnp.arange(block_count))
    )
    return (grad_queries.reshape(half_len, head_count, head_size), sums[0], sums[1])


def scatter_low(grad, dim):
    summed = lax.psum_scatter(
        grad.astype(jnp.bfloat16), ("shard", "ctx"), scatter_dimension=dim, tiled=True
    )
    return summed.astype(jnp.float32)


def matmul_low(left, right):
    return jnp.dot(left, right, preferred_element_type=jnp.float32)


def body(tokens, lengths, cotangent, w_query, w_key, w_value, w_output, w_gate, w_up, w_down):
    seq_count, half_len, model_width = tokens.shape
    head_cols = w_query.shape[1]
    head_count = head_cols // HEAD_DIM
    row_total = seq_count * half_len
    offset = lax.axis_index("ctx") * half_len
    positions = offset + jnp.arange(half_len)
    valid_mask = (positions[None, :] < lengths[:, None]).astype(jnp.float32)
    bf_type = jnp.bfloat16
    attn_low = (
        w_query.astype(bf_type),
        w_key.astype(bf_type),
        w_value.astype(bf_type),
        w_output.astype(bf_type),
    )
    mlp_low = (w_gate.astype(bf_type), w_up.astype(bf_type), w_down.astype(bf_type))
    query_full, key_full, value_full, output_full = (
        lax.all_gather(attn_low[0], ("shard", "ctx"), axis=0, tiled=True),
        lax.all_gather(attn_low[1], ("shard", "ctx"), axis=0, tiled=True),
        lax.all_gather(attn_low[2], ("shard", "ctx"), axis=0, tiled=True),
        lax.all_gather(attn_low[3], ("shard", "ctx"), axis=1, tiled=True),
    )
    gate_full, up_full, down_full = (
        lax.all_gather(mlp_low[0], ("shard", "ctx"), axis=0, tiled=True),
        lax.all_gather(mlp_low[1], ("shard", "ctx"), axis=0, tiled=True),
        lax.all_gather(mlp_low[2], ("shard", "ctx"), axis=1, tiled=True),
    )
    tokens_wide = tokens.astype(jnp.float32).reshape(row_total, model_width)
    normed_one, scale_one = normalize(tokens_wide)
    input_one = normed_one.astype(bf_type)
    split_heads = (seq_count, half_len, head_count, HEAD_DIM)
    query_pre = matmul_low(input_one, query_full).reshape(split_heads)
    key_pre = matmul_low(input_one, key_full).reshape(split_heads)
    value_pre = matmul_low(input_one, value_full).reshape(split_heads)
    cosine, sine_table = rope_tables(half_len, HEAD_DIM, offset)
    queries = rotate(query_pre, cosine, sine_table).astype(bf_type)
    keys_rot = rotate(key_pre, cosine, sine_table).astype(bf_type)
    values_low = value_pre.astype(bf_type)
    keys_all, values_all = (
        lax.all_gather(keys_rot, "ctx", axis=1, tiled=True),
        lax.all_gather(values_low, "ctx", axis=1, tiled=True),
    )
    seq_index = 0
    attended, log_totals = attend_forward(
        queries[seq_index], keys_all[seq_index], values_all[seq_index], lengths[seq_index], offset
    )
    attended_list = [attended]
    log_list = [log_totals]
    attn_out = jnp.stack(attended_list).reshape(row_total, head_cols)
    branch_part = matmul_low(attn_out, output_full)
    resid = tokens_wide + lax.psum(branch_part.astype(bf_type), "tp").astype(jnp.float32)
    normed_two, scale_two = normalize(resid)
    input_two = normed_two.astype(bf_type)
    gate_proj = matmul_low(input_two, gate_full)
    up_proj = matmul_low(input_two, up_full)
    gate_sigmoid = jax.nn.sigmoid(gate_proj)
    hidden = (gate_proj * gate_sigmoid * up_proj).astype(bf_type)
    branch_two_part = matmul_low(hidden, down_full)
    final_sum = resid + lax.psum(branch_two_part.astype(jnp.bfloat16), "tp").astype(jnp.float32)
    grad_final = cotangent.astype(jnp.float32).reshape(row_total, model_width) * valid_mask.reshape(
        row_total, 1
    )
    grad_branch = grad_final.astype(bf_type)
    grad_down = jnp.einsum("rf,rd->fd", hidden, grad_branch, preferred_element_type=jnp.float32)
    grad_hidden = jnp.einsum(
        "rd,fd->rf", grad_branch, down_full, preferred_element_type=jnp.float32
    )
    grad_gate_act = (
        grad_hidden * up_proj * gate_sigmoid * (1.0 + gate_proj * (1.0 - gate_sigmoid))
    ).astype(bf_type)
    grad_up_act = (grad_hidden * gate_proj * gate_sigmoid).astype(bf_type)
    grad_gate = jnp.einsum(
        "rd,rf->df", input_two, grad_gate_act, preferred_element_type=jnp.float32
    )
    grad_up = jnp.einsum("rd,rf->df", input_two, grad_up_act, preferred_element_type=jnp.float32)
    grad_input_two = jnp.einsum(
        "rf,df->rd", grad_gate_act, gate_full, preferred_element_type=jnp.float32
    ) + jnp.einsum("rf,df->rd", grad_up_act, up_full, preferred_element_type=jnp.float32)
    mlp_grads = (scatter_low(grad_gate, 0), scatter_low(grad_up, 0), scatter_low(grad_down, 1))
    grad_input_two = lax.psum(grad_input_two.astype(bf_type), "tp").astype(jnp.float32)
    grad_resid = grad_final + norm_back(normed_two, scale_two, grad_input_two)
    grad_resid_low = grad_resid.astype(bf_type)
    grad_wout = jnp.einsum(
        "rc,rd->cd", attn_out, grad_resid_low, preferred_element_type=jnp.float32
    )
    grad_attn = jnp.einsum(
        "rd,cd->rc", grad_resid_low, output_full, preferred_element_type=jnp.float32
    )
    grad_attn = grad_attn.astype(bf_type).reshape(split_heads)
    seq_index = 0
    grad_queries, grad_keys_seq, grad_values_seq = attend_backward(
        queries[seq_index],
        keys_all[seq_index],
        values_all[seq_index],
        lengths[seq_index],
        offset,
        log_list[seq_index],
        grad_attn[seq_index],
    )
    query_grads = [grad_queries]
    key_grads = [grad_keys_seq]
    value_grads = [grad_values_seq]
    grad_keys, grad_values = (
        lax.psum_scatter(jnp.stack(key_grads), "ctx", scatter_dimension=1, tiled=True),
        lax.psum_scatter(jnp.stack(value_grads), "ctx", scatter_dimension=1, tiled=True),
    )
    grad_q_pre = (
        rotate_back(jnp.stack(query_grads), cosine, sine_table)
        .astype(bf_type)
        .reshape(row_total, head_cols)
    )
    grad_k_pre = (
        rotate_back(grad_keys, cosine, sine_table).astype(bf_type).reshape(row_total, head_cols)
    )
    grad_v_pre = grad_values.astype(bf_type).reshape(row_total, head_cols)
    grad_wq = jnp.einsum("rd,rc->dc", input_one, grad_q_pre, preferred_element_type=jnp.float32)
    grad_wk = jnp.einsum("rd,rc->dc", input_one, grad_k_pre, preferred_element_type=jnp.float32)
    grad_wv = jnp.einsum("rd,rc->dc", input_one, grad_v_pre, preferred_element_type=jnp.float32)
    grad_input_one = (
        jnp.einsum("rc,dc->rd", grad_q_pre, query_full, preferred_element_type=jnp.float32)
        + jnp.einsum("rc,dc->rd", grad_k_pre, key_full, preferred_element_type=jnp.float32)
        + jnp.einsum("rc,dc->rd", grad_v_pre, value_full, preferred_element_type=jnp.float32)
    )
    attn_grads = (
        scatter_low(grad_wq, 0),
        scatter_low(grad_wk, 0),
        scatter_low(grad_wv, 0),
        scatter_low(grad_wout, 1),
    )
    grad_input_one = lax.psum(grad_input_one.astype(bf_type), "tp").astype(jnp.float32)
    grad_tokens = grad_resid + norm_back(normed_one, scale_one, grad_input_one)
    output = final_sum.astype(bf_type).reshape(seq_count, half_len, model_width)
    grad_tokens = grad_tokens.reshape(seq_count, half_len, model_width)
    return (
        output,
        grad_tokens,
        attn_grads[0],
        attn_grads[1],
        attn_grads[2],
        attn_grads[3],
        mlp_grads[0],
        mlp_grads[1],
        mlp_grads[2],
    )


def solution(mesh):
    return jax.shard_map(
        body,
        mesh=mesh,
        in_specs=(
            P("shard", "ctx", None),
            P("shard"),
            P("shard", "ctx", None),
            P(("shard", "ctx"), "tp"),
            P(("shard", "ctx"), "tp"),
            P(("shard", "ctx"), "tp"),
            P("tp", ("shard", "ctx")),
            P(("shard", "ctx"), "tp"),
            P(("shard", "ctx"), "tp"),
            P("tp", ("shard", "ctx")),
        ),
        out_specs=(
            P("shard", "ctx", None),
            P("shard", "ctx", None),
            P(("shard", "ctx"), "tp"),
            P(("shard", "ctx"), "tp"),
            P(("shard", "ctx"), "tp"),
            P("tp", ("shard", "ctx")),
            P(("shard", "ctx"), "tp"),
            P(("shard", "ctx"), "tp"),
            P("tp", ("shard", "ctx")),
        ),
        check_vma=False,
    )
```

profile of v0, /device:TPU:0, one launch (start us, length us, event | category | flops | bytes accessed | tf_op | source)
XLA Modules:
  0.0 1603.9 jit_solution(9619642317359347338)
XLA Ops:
  21.9 19.1 %all-gather.13.cloned.1.call-done = bf16[2048,512]{1,0:T(8,128)(2,1)} async-done(((bf16[256,512]{1,0:T(8,128)(2,1)}), bf16[2048,512]{1,0:T(8,128)(2,1)}) %all-gather.13.cloned.1.call-update) | async-done | bytes 2097168 | tf_op jit(solution)/shard_map/all_gather | solution.py:142
  41.0 5.2 fusion.112
  48.2 23.1 %all-gather.17.cloned.1.call-done = bf16[2048,512]{1,0:T(8,128)(2,1)} async-done(((bf16[256,512]{1,0:T(8,128)(2,1)}), bf16[2048,512]{1,0:T(8,128)(2,1)}) %all-gather.17.cloned.1.call-update) | async-done | bytes 2097168 | tf_op jit(solution)/shard_map/all_gather | solution.py:143
  74.2 5.6 fusion.89
  84.3 17.2 %all-gather.11.cloned.1.call-done = bf16[2048,512]{1,0:T(8,128)(2,1)} async-done(((bf16[256,512]{1,0:T(8,128)(2,1)}), bf16[2048,512]{1,0:T(8,128)(2,1)}) %all-gather.11.cloned.1.call-update) | async-done | bytes 2097168 | tf_op jit(solution)/shard_map/all_gather | solution.py:141
  101.5 6.6 fusion.111
  131.7 34.9 %while.27 = (s32[]{:T(128)}, bf16[2,512,4,128]{3,2,1,0:T(4,128)(2,1)}, f32[2,4,512]{2,1,0:T(4,128)S(1)}, s32[2]{0:T(128)S(1)}, s32[]{:T(128)}, /*index=5*/s32[]{...) while((s32[]{:T(128)}, ...), condition=%wide.region_5.6_spmd, body=%wide.region_2.5_spmd.sunk | while | flops 2195980800 | bytes 77668600 | solution.py:71
  142.4 5.3 fusion.174
  159.8 5.3 fusion.174
  166.6 6.3 convolution_convert_fusion.4
  182.3 146.1 %all-reduce.5.cloned.1.call-done = bf16[1024,2048]{1,0:T(8,128)(2,1)} async-done(((bf16[1024,2048]{1,0:T(8,128)(2,1)}), bf16[1024,2048]{1,0:T(8,128)(2,1)}) %all-reduce.5.cloned.1.call-update) | async-done | bytes 4194320 | tf_op jit(solution)/shard_map/psum | solution.py:174
  339.8 44.3 %all-gather.21.cloned.1.call-done = bf16[2048,2048]{1,0:T(8,128)(2,1)} async-done(((bf16[256,2048]{1,0:T(8,128)(2,1)}), bf16[2048,2048]{1,0:T(8,128)(2,1)}) %all-gather.21.cloned.1.call-update) | async-done | bytes 8388624 | tf_op jit(solution)/shard_map/all_gather | solution.py:147
  384.1 14.5 fusion.113
  398.6 42.3 %all-gather.23.cloned.1.call-done = bf16[2048,2048]{1,0:T(8,128)(2,1)} async-done(((bf16[256,2048]{1,0:T(8,128)(2,1)}), bf16[2048,2048]{1,0:T(8,128)(2,1)}) %all-gather.23.cloned.1.call-update) | async-done | bytes 8388624 | tf_op jit(solution)/shard_map/all_gather | solution.py:148
  440.9 14.5 fusion.114
  455.4 43.6 %all-gather.25.cloned.1.call-done = bf16[2048,2048]{1,0:T(8,128)(2,1)} async-done(((bf16[2048,256]{1,0:T(8,128)(2,1)}), bf16[2048,2048]{1,0:T(8,128)(2,1)}) %all-gather.25.cloned.1.call-update) | async-done | bytes 8388624 | tf_op jit(solution)/shard_map/all_gather | solution.py:149
  499.1 22.3 %multiply_convert_fusion.1 = (bf16[1024,2048]{1,0:T(8,128)(2,1)}, bf16[1024,2048]{1,0:T(8,128)(2,1)}, bf16[1024,2048]{1,0:T(8,128)(2,1)}) fusion(f32[1024,2048]{1,0:T(8,128)} %fusion.113, f32[1024,2048]{1,0:T(8,128)} %fusion.114, bf16[2048,2048]{1,0:T(8,128)(2,1)} %all-gather.25.cloned.1.call-done, bf16[1,1024,2048]{2,1,0:T(8,128)(2,1)} %param.16, ...), kind=kOutput, calls=%fused_computation.80 | convolution fusion | flops 8629780480 | bytes 41947136 | tf_op jit(solution)/shard_map/rd,fd->rf/dot_general | solution.py:188
  521.3 14.7 fusion.115
  536.0 12.2 add_convert_fusion.1
  548.3 155.1 %all-reduce.7.cloned.1.call-done = bf16[1024,2048]{1,0:T(8,128)(2,1)} async-done(((bf16[1024,2048]{1,0:T(8,128)(2,1)}), bf16[1024,2048]{1,0:T(8,128)(2,1)}) %all-reduce.7.cloned.1.call-update) | async-done | bytes 4194320 | tf_op jit(solution)/shard_map/psum | solution.py:203
  703.4 8.3 convert_reduce_fusion.1
  711.8 6.1 fusion.46
  726.7 127.9 %while.28 = (s32[]{:T(128)}, f32[2048,4,128]{0,2,1:T(8,128)}, f32[2048,4,128]{0,2,1:T(8,128)}, f32[2,512,4,128]{3,1,2,0:T(8,128)}, bf16[2,512,4,128]{3,1,2,0:T(8...) while((s32[]{:T(128)}, f32[2048,4,128]{0,2,1:T(8,128)}, ...), condition=%wide.region_15.16_spmd.clone, body=%wide.region_13.15_spmd.clone.sunk | while | flops 5439226368 | bytes 211878384 | solution.py:107
  726.9 8.2 fusion.183
  739.1 13.2 multiply_reduce_fusion.3
  752.2 14.9 multiply_convert_fusion.5
  767.1 7.4 bitcast_add_fusion.4
  774.5 11.2 bitcast_add_fusion.5
  789.5 8.1 fusion.183
  801.6 13.2 multiply_reduce_fusion.3
  814.8 14.9 multiply_convert_fusion.5
  829.7 8.6 bitcast_add_fusion.4
  838.3 12.4 bitcast_add_fusion.5
  865.9 7.1 convolution_convert_fusion.5
  873.1 15.2 convolution_convert_fusion.2
  888.3 14.0 convolution_convert_fusion.1
  903.0 14.5 convolution_convert_fusion
  931.0 6.6 fusion.61
  937.6 14.5 convolution_convert_fusion.3
  960.6 5.8 add_convert_fusion
  973.9 73.1 %reduce-scatter.22.cloned.1.call-done = bf16[256,2048]{1,0:T(8,128)(2,1)} async-done(((bf16[2048,2048]{1,0:T(8,128)(2,1)}), bf16[256,2048]{1,0:T(8,128)(2,1)}) %reduce-scatter.22.cloned.1.call-update) | async-done | bytes 1048592 | tf_op jit(solution)/shard_map/reduce_scatter | solution.py:114
  1049.8 72.1 %reduce-scatter.24.cloned.1.call-done = bf16[256,2048]{1,0:T(8,128)(2,1)} async-done(((bf16[2048,2048]{1,0:T(8,128)(2,1)}), bf16[256,2048]{1,0:T(8,128)(2,1)}) %reduce-scatter.24.cloned.1.call-update) | async-done | bytes 1048592 | tf_op jit(solution)/shard_map/reduce_scatter | solution.py:114
  1124.7 71.9 %reduce-scatter.26.cloned.1.call-done = bf16[2048,256]{1,0:T(8,128)(2,1)} async-done(((bf16[2048,2048]{1,0:T(8,128)(2,1)}), bf16[2048,256]{1,0:T(8,128)(2,1)}) %reduce-scatter.26.cloned.1.call-update) | async-done | bytes 1048592 | tf_op jit(solution)/shard_map/reduce_scatter | solution.py:114
  1199.2 41.7 %reduce-scatter.16.cloned.1.call-done = bf16[256,512]{1,0:T(8,128)(2,1)} async-done(((bf16[2048,512]{1,0:T(8,128)(2,1)}), bf16[256,512]{1,0:T(8,128)(2,1)}) %reduce-scatter.16.cloned.1.call-update) | async-done | bytes 262160 | tf_op jit(solution)/shard_map/reduce_scatter | solution.py:114
  1242.7 42.5 %reduce-scatter.18.cloned.1.call-done = bf16[256,512]{1,0:T(8,128)(2,1)} async-done(((bf16[2048,512]{1,0:T(8,128)(2,1)}), bf16[256,512]{1,0:T(8,128)(2,1)}) %reduce-scatter.18.cloned.1.call-update) | async-done | bytes 262160 | tf_op jit(solution)/shard_map/reduce_scatter | solution.py:114
  1287.0 292.3 %all-reduce.9.cloned.1.call-done = (bf16[1024,2048]{1,0:T(8,128)(2,1)}, bf16[1024,2048]{1,0:T(8,128)(2,1)}) async-done(((bf16[1024,2048]{1,0:T(8,128)(2,1)}, bf16[1024,2048]{1,0:T(8,128)(2,1)}), (bf16[1024,2048]{1,0:T(8,128)(2,1)}, bf16[1024,2048]{1,0:T(8,128)(2,1)})) %all-reduce.9.cloned.1.call-update) | async-done | bytes 8388624 | tf_op jit(solution)/shard_map/psum | solution.py:182
  1579.3 6.7 convert_reduce_fusion
  1586.1 10.5 fusion.40
  (281 shorter events, 166.2 us)
Async XLA Ops:
  7.2 33.8 %all-gather.13.cloned.1.call-start = ((), (), s32[]{:S(2)}) async-start(), calls=%async_computation.10 | async-start | bytes 2359296 | tf_op jit(solution)/shard_map/all_gather | solution.py:142
  9.0 62.2 %all-gather.17.cloned.1.call-start = ((), (), s32[]{:S(2)}) async-start(), calls=%async_computation.12 | async-start | bytes 2359296 | tf_op jit(solution)/shard_map/all_gather | solution.py:143
  10.9 90.6 %all-gather.11.cloned.1.call-start = ((), (), s32[]{:S(2)}) async-start(), calls=%async_computation.9 | async-start | bytes 2359296 | tf_op jit(solution)/shard_map/all_gather | solution.py:141
  12.7 115.8 %all-gather.15.cloned.1.call-start = ((), (), s32[]{:S(2)}) async-start(), calls=%async_computation.11 | async-start | bytes 3145728 | tf_op jit(solution)/shard_map/all_gather | solution.py:163
  14.8 31.7 %copy-start.23 = (f32[1024,128]{0,1:T(8,128)}, f32[1024,128]{0,1:T(8,128)S(1)}, u32[]{:S(2)}) copy-start(f32[1024,128]{0,1:T(8,128)S(1)} %get-tuple-element.318) | copy-start | bytes 1572868
  14.8 31.7 %copy-start.25 = (f32[1024,128]{0,1:T(8,128)}, f32[1024,128]{0,1:T(8,128)S(1)}, u32[]{:S(2)}) copy-start(f32[1024,128]{0,1:T(8,128)S(1)} %get-tuple-element.319) | copy-start | bytes 1572868
  18.0 56.2 %copy-start.38 = (f32[1024]{0:T(1024)}, f32[1024]{0:T(1024)S(1)}, u32[]{:S(2)}) copy-start(f32[1024]{0:T(1024)S(1)} %broadcast_multiply_fusion.7) | copy-start | bytes 12292
  19.3 54.9 %copy-start.42 = (f32[1024]{0:T(1024)}, f32[1024]{0:T(1024)S(1)}, u32[]{:S(2)}) copy-start(f32[1024]{0:T(1024)S(1)} %add_rsqrt_fusion.1) | copy-start | bytes 12292
  48.1 83.5 %all-gather.27.cloned.1.call-start = ((), (), s32[]{:S(2)}) async-start(), calls=%async_computation.28 | async-start | bytes 3145728 | tf_op jit(solution)/shard_map/all_gather | solution.py:164
  79.8 86.7 %all-gather.19.cloned.1.call-start = ((), (), s32[]{:S(2)}) async-start(), calls=%async_computation.13 | async-start | bytes 2359296 | tf_op jit(solution)/shard_map/all_gather | solution.py:144
  80.7 247.7 %all-reduce.5.cloned.1.call-start = ((), (), s32[]{:S(2)}) async-start(), calls=%async_computation.14 | async-start | bytes 8388608 | tf_op jit(solution)/shard_map/psum | solution.py:174
  166.6 6.3 copy-start.40
  172.9 211.2 %all-gather.21.cloned.1.call-start = ((), (), s32[]{:S(2)}) async-start(), calls=%async_computation.15 | async-start | bytes 9437184 | tf_op jit(solution)/shard_map/all_gather | solution.py:147
  175.7 265.2 %all-gather.23.cloned.1.call-start = ((), (), s32[]{:S(2)}) async-start(), calls=%async_computation.16 | async-start | bytes 9437184 | tf_op jit(solution)/shard_map/all_gather | solution.py:148
  178.5 320.6 %all-gather.25.cloned.1.call-start = ((), (), s32[]{:S(2)}) async-start(), calls=%async_computation.17 | async-start | bytes 9437184 | tf_op jit(solution)/shard_map/all_gather | solution.py:149
  181.6 521.8 %all-reduce.7.cloned.1.call-start = ((), (), s32[]{:S(2)}) async-start(), calls=%async_computation.18 | async-start | bytes 8388608 | tf_op jit(solution)/shard_map/psum | solution.py:203
  182.3 529.4 %copy-start.44 = (f32[1024]{0:T(1024)}, f32[1024]{0:T(1024)S(1)}, u32[]{:S(2)}) copy-start(f32[1024]{0:T(1024)S(1)} %fusion.106) | copy-start | bytes 12292
  328.4 5.9 copy-start.6
  521.3 14.7 copy-start.46
  521.3 14.7 copy-start.49
  548.2 369.4 %reduce-scatter.10.cloned.1.call-start = ((), (), s32[]{:S(2)}) async-start(), calls=%async_computation.19 | async-start | bytes 6291456 | tf_op jit(solution)/shard_map/reduce_scatter | solution.py:227
  703.4 8.4 copy-start.2
  703.4 8.4 copy-start.7
  703.4 8.4 copy-start.20
  711.8 9.5 copy-start.48
  726.9 8.2 copy-start.9
  739.1 13.2 copy-start.12
  767.1 7.4 copy-start.13
  767.1 18.7 %slice-start = ((s8[8388608]{0:T(1024)(128)(4,1)}), s8[4194304]{0:T(1024)(128)(4,1)S(1)}, s32[]{:S(2)}) async-start(s8[8388608]{0:T(1024)(128)(4,1)} %bitcast.246), calls=%async_computation.30 | async-start | bytes 8388608 | tf_op jit(solution)/shard_map/while
  774.5 11.2 slice-start.1
  774.5 11.3 copy-start.15
  789.5 8.1 copy-start.9
  801.6 13.2 copy-start.12
  829.7 8.6 copy-start.13
  829.7 21.1 %slice-start = ((s8[8388608]{0:T(1024)(128)(4,1)}), s8[4194304]{0:T(1024)(128)(4,1)S(1)}, s32[]{:S(2)}) async-start(s8[8388608]{0:T(1024)(128)(4,1)} %bitcast.246), calls=%async_computation.30 | async-start | bytes 8388608 | tf_op jit(solution)/shard_map/while
  838.3 12.4 slice-start.1
  838.3 12.4 copy-start.15
  854.7 73.6 %reduce-scatter.12.cloned.1.call-start = ((), (), s32[]{:S(2)}) async-start(), calls=%async_computation.20 | async-start | bytes 6291456 | tf_op jit(solution)/shard_map/reduce_scatter | solution.py:228
  855.4 111.1 %reduce-scatter.14.cloned.1.call-start = ((), (), s32[]{:S(2)}) async-start(), calls=%async_computation.21 | async-start | bytes 2359296 | tf_op jit(solution)/shard_map/reduce_scatter | solution.py:114
  865.8 106.3 %reduce-scatter.20.cloned.1.call-start = ((), (), s32[]{:S(2)}) async-start(), calls=%async_computation.24 | async-start | bytes 2359296 | tf_op jit(solution)/shard_map/reduce_scatter | solution.py:114
  873.0 174.0 %reduce-scatter.22.cloned.1.call-start = ((), (), s32[]{:S(2)}) async-start(), calls=%async_computation.25 | async-start | bytes 9437184 | tf_op jit(solution)/shard_map/reduce_scatter | solution.py:114
  888.2 233.6 %reduce-scatter.24.cloned.1.call-start = ((), (), s32[]{:S(2)}) async-start(), calls=%async_computation.26 | async-start | bytes 9437184 | tf_op jit(solution)/shard_map/reduce_scatter | solution.py:114
  902.3 294.2 %reduce-scatter.26.cloned.1.call-start = ((), (), s32[]{:S(2)}) async-start(), calls=%async_computation.27 | async-start | bytes 9437184 | tf_op jit(solution)/shard_map/reduce_scatter | solution.py:114
  917.5 323.4 %reduce-scatter.16.cloned.1.call-start = ((), (), s32[]{:S(2)}) async-start(), calls=%async_computation.22 | async-start | bytes 2359296 | tf_op jit(solution)/shard_map/reduce_scatter | solution.py:114
  926.8 358.4 %reduce-scatter.18.cloned.1.call-start = ((), (), s32[]{:S(2)}) async-start(), calls=%async_computation.23 | async-start | bytes 2359296 | tf_op jit(solution)/shard_map/reduce_scatter | solution.py:114
  937.6 641.7 %all-reduce.9.cloned.1.call-start = ((), (), s32[]{:S(2)}) async-start(), calls=%async_computation.29 | async-start | bytes 16777216 | tf_op jit(solution)/shard_map/psum | solution.py:182
  1579.3 6.8 copy-start.5
  1579.3 6.8 copy-start.8
  (36 other events, 101.3 us)
Sparse Core Ops, SparseCore 0:
  10.4 30.4 all-gather.12
  43.4 27.7 all-gather.16
  73.7 27.7 all-gather.10
  103.5 10.5 all-gather.14
  115.5 11.7 all-gather.26
  129.0 29.2 all-gather.18
  173.0 155.3 all-reduce.4
  330.8 53.2 all-gather.20
  386.6 54.2 all-gather.22
  443.2 55.8 all-gather.24
  548.4 154.9 all-reduce.6
  854.8 10.8 reduce-scatter.9
  867.9 13.1 reduce-scatter.11
  884.9 42.3 reduce-scatter.13
  931.0 41.1 reduce-scatter.19
  975.5 71.4 reduce-scatter.21
  1050.3 71.5 reduce-scatter.23
  1125.2 71.2 reduce-scatter.25
  1199.8 41.0 reduce-scatter.15
  1244.1 41.0 reduce-scatter.17
  1288.4 290.8 all-reduce.8
where the time goes:
time: 1610 us; the launch traced here: 1600 us
  waiting for transfers between devices  1090 us (68%)
  matrix products  301 us (19%)
  other arithmetic  143 us (9%)
  local copies, waits for them, and re-layouts  49.4 us (3%)
  between operations  16.3 us (1%)
    reduce_scatter x7, waiting for transfers between devices, scatter_low(): lax.psum_scatter(grad.astype(jnp.bfloat16), ('shard', 'ctx'), scatter_dim...  305 us
    psum x1, waiting for transfers between devices, body(): lax.psum(branch_two_part.astype(jnp.bfloat16), 'tp').astype(jnp.float32)  292 us
    psum x1, waiting for transfers between devices, body(): lax.psum(grad_input_two.astype(bf_type), 'tp').astype(jnp.float32)  155 us
    psum x1, waiting for transfers between devices, body(): lax.psum(branch_part.astype(bf_type), 'tp').astype(jnp.float32)  146 us
    dot_general x7, matrix products, matmul_low(): return jnp.dot(left, right, preferred_element_type=jnp.float32)  67.1 us
    all_gather x1, waiting for transfers between devices, body(): lax.all_gather(mlp_low[0], ('shard', 'ctx'), axis=0, tiled=True)  44.3 us
    all_gather x1, waiting for transfers between devices, body(): lax.all_gather(mlp_low[2], ('shard', 'ctx'), axis=1, tiled=True)  43.6 us
    all_gather x1, waiting for transfers between devices, body(): lax.all_gather(mlp_low[1], ('shard', 'ctx'), axis=0, tiled=True)  42.3 us
  transfers between devices with their start and end apart: 21, of which 15 were waited for; matrix products, arithmetic and copies ran while one was open for 16% of the time, Pallas kernels for 0%

commit v1 on v0

--- a/solution.py
+++ b/solution.py
@@ -1,3 +1,4 @@
+import functools
 import jax
 import jax.numpy as jnp
 from jax import lax
@@ -5,6 +6,14 @@
 
 HEAD_DIM = 128
 EPSILON = 1e-05
+
+
+def thing_solve(incoming_x, named_axis):
+    val2 = lax.all_gather(incoming_x, axis_name=named_axis)
+    return jnp.sum(val2, 0)
+
+
+play_kinds_on_mesh = functools.partial(thing_solve, named_axis="tp")
 
 
 def normalize(values):
@@ -200,7 +209,7 @@
         "rf,df->rd", grad_gate_act, gate_full, preferred_element_type=jnp.float32
     ) + jnp.einsum("rf,df->rd", grad_up_act, up_full, preferred_element_type=jnp.float32)
     mlp_grads = (scatter_low(grad_gate, 0), scatter_low(grad_up, 0), scatter_low(grad_down, 1))
-    grad_input_two = lax.psum(grad_input_two.astype(bf_type), "tp").astype(jnp.float32)
+    grad_input_two = play_kinds_on_mesh(grad_input_two.astype(bf_type)).astype(jnp.float32)
     grad_resid = grad_final + norm_back(normed_two, scale_two, grad_input_two)
     grad_resid_low = grad_resid.astype(bf_type)
     grad_wout = jnp.einsum(

time: 1610 us -> 1750 us (1.087)
  waiting for transfers between devices: 1090 us -> 1220 us
    all_gather x0 -> x1, waiting for transfers between devices: none -> 287 us  [thing_solve(): val2 = lax.all_gather(incoming_x, axis_name=named_axis)]
    psum x1 -> x0, waiting for transfers between devices: 155 us -> none  [body(): lax.psum(grad_input_two.astype(bf_type), 'tp').astype(jnp.float32)]
  transfers between devices with their start and end apart: 21 -> 21, of which waited for: 15 -> 15; matrix products, arithmetic and copies ran while one was open for 16% -> 15% of each run, Pallas kernels for 0% -> 0%
where the time goes in v1:
time: 1750 us
  waiting for transfers between devices  1220 us (70%)
  matrix products  300 us (17%)
  other arithmetic  156 us (9%)
  local copies, waits for them, and re-layouts  49.6 us (3%)
    reduce_scatter x7, waiting for transfers between devices, scatter_low(): lax.psum_scatter(grad.astype(jnp.bfloat16), ('shard', 'ctx'), scatter_dim...  304 us
    psum x1, waiting for transfers between devices, body(): lax.psum(branch_two_part.astype(jnp.bfloat16), 'tp').astype(jnp.float32)  292 us
    all_gather x1, waiting for transfers between devices, thing_solve(): val2 = lax.all_gather(incoming_x, axis_name=named_axis)  287 us
    psum x1, waiting for transfers between devices, body(): lax.psum(branch_part.astype(bf_type), 'tp').astype(jnp.float32)  146 us
    dot_general x7, matrix products, matmul_low(): return jnp.dot(left, right, preferred_element_type=jnp.float32)  66.9 us
    all_gather x1, waiting for transfers between devices, body(): lax.all_gather(mlp_low[0], ('shard', 'ctx'), axis=0, tiled=True)  44.3 us
    all_gather x1, waiting for transfers between devices, body(): lax.all_gather(mlp_low[2], ('shard', 'ctx'), axis=1, tiled=True)  43.6 us
    all_gather x1, waiting for transfers between devices, body(): lax.all_gather(mlp_low[1], ('shard', 'ctx'), axis=0, tiled=True)  42.3 us
  transfers between devices with their start and end apart: 21, of which 15 were waited for; matrix products, arithmetic and copies ran while one was open for 15% of the time, Pallas kernels for 0%

profile of v1, /device:TPU:0, one launch (start us, length us, event | category | flops | bytes accessed | tf_op | source)
XLA Modules:
  0.0 1745.7 jit_solution(18435968540365722762)
XLA Ops:
  21.9 19.1 %all-gather.15.cloned.1.call-done = bf16[2048,512]{1,0:T(8,128)(2,1)} async-done(((bf16[256,512]{1,0:T(8,128)(2,1)}), bf16[2048,512]{1,0:T(8,128)(2,1)}) %all-gather.15.cloned.1.call-update) | async-done | bytes 2097168 | tf_op jit(solution)/shard_map/all_gather | solution.py:151
  48.2 23.1 %all-gather.19.cloned.1.call-done = bf16[2048,512]{1,0:T(8,128)(2,1)} async-done(((bf16[256,512]{1,0:T(8,128)(2,1)}), bf16[2048,512]{1,0:T(8,128)(2,1)}) %all-gather.19.cloned.1.call-update) | async-done | bytes 2097168 | tf_op jit(solution)/shard_map/all_gather | solution.py:152
  74.2 5.6 fusion.89
  84.3 17.2 all-gather.13.cloned.1.call-done
  101.5 6.6 fusion.111
  131.7 34.9 %while.27 = (s32[]{:T(128)}, bf16[2,512,4,128]{3,2,1,0:T(4,128)(2,1)}, f32[2,4,512]{2,1,0:T(4,128)S(1)}, s32[2]{0:T(128)S(1)}, s32[]{:T(128)}, /*index=5*/s32[]{...) while((s32[]{:T(128)}, ...), condition=%wide.region_5.6_spmd, body=%wide.region_2.5_spmd.sunk | while | flops 2195980800 | bytes 77668600 | solution.py:80
  142.4 5.3 fusion.174
  166.6 6.3 convolution_convert_fusion.4
  182.3 146.1 %all-reduce.4.cloned.1.call-done = bf16[1024,2048]{1,0:T(8,128)(2,1)} async-done(((bf16[1024,2048]{1,0:T(8,128)(2,1)}), bf16[1024,2048]{1,0:T(8,128)(2,1)}) %all-reduce.4.cloned.1.call-update) | async-done | bytes 4194320 | tf_op jit(solution)/shard_map/psum | solution.py:183
  339.8 44.3 %all-gather.23.cloned.1.call-done = bf16[2048,2048]{1,0:T(8,128)(2,1)} async-done(((bf16[256,2048]{1,0:T(8,128)(2,1)}), bf16[2048,2048]{1,0:T(8,128)(2,1)}) %all-gather.23.cloned.1.call-update) | async-done | bytes 8388624 | tf_op jit(solution)/shard_map/all_gather | solution.py:156
  384.1 14.5 fusion.113
  398.6 42.3 %all-gather.25.cloned.1.call-done = bf16[2048,2048]{1,0:T(8,128)(2,1)} async-done(((bf16[256,2048]{1,0:T(8,128)(2,1)}), bf16[2048,2048]{1,0:T(8,128)(2,1)}) %all-gather.25.cloned.1.call-update) | async-done | bytes 8388624 | tf_op jit(solution)/shard_map/all_gather | solution.py:157
  440.9 14.5 fusion.114
  455.4 43.6 %all-gather.27.cloned.1.call-done = bf16[2048,2048]{1,0:T(8,128)(2,1)} async-done(((bf16[2048,256]{1,0:T(8,128)(2,1)}), bf16[2048,2048]{1,0:T(8,128)(2,1)}) %all-gather.27.cloned.1.call-update) | async-done | bytes 8388624 | tf_op jit(solution)/shard_map/all_gather | solution.py:158
  499.1 22.3 %multiply_convert_fusion.1 = (bf16[1024,2048]{1,0:T(8,128)(2,1)}, bf16[1024,2048]{1,0:T(8,128)(2,1)}, bf16[1024,2048]{1,0:T(8,128)(2,1)}) fusion(f32[1024,2048]{1,0:T(8,128)} %fusion.113, f32[1024,2048]{1,0:T(8,128)} %fusion.114, bf16[2048,2048]{1,0:T(8,128)(2,1)} %all-gather.27.cloned.1.call-done, bf16[1,1024,2048]{2,1,0:T(8,128)(2,1)} %param.16, ...), kind=kOutput, calls=%fused_computation.80 | convolution fusion | flops 8629780480 | bytes 41947136 | tf_op jit(solution)/shard_map/rd,fd->rf/dot_general | solution.py:197
  521.3 14.7 fusion.115
  536.0 12.2 add_convert_fusion.1
  548.3 286.8 %all-gather.31.cloned.1.call-done = bf16[4096,2048]{1,0:T(8,128)(2,1)} async-done(((bf16[1024,2048]{1,0:T(8,128)(2,1)}), bf16[4096,2048]{1,0:T(8,128)(2,1)}) %all-gather.31.cloned.1.call-update) | async-done | bytes 16777232 | tf_op jit(solution)/shard_map/all_gather | solution.py:12
  835.1 12.3 reduce_sum.106
  847.4 8.4 convert_reduce_fusion.1
  855.9 6.1 fusion.46
  870.9 127.9 %while.28 = (s32[]{:T(128)}, f32[2048,4,128]{0,2,1:T(8,128)}, f32[2048,4,128]{0,2,1:T(8,128)}, f32[2,512,4,128]{3,1,2,0:T(8,128)}, bf16[2,512,4,128]{3,1,2,0:T(8...) while((s32[]{:T(128)}, f32[2048,4,128]{0,2,1:T(8,128)}, ...), condition=%wide.region_15.16_spmd.clone, body=%wide.region_13.15_spmd.clone.sunk | while | flops 5439226368 | bytes 211878384 | solution.py:116
  870.9 8.2 fusion.183
  883.0 13.2 multiply_reduce_fusion.3
  896.2 14.9 multiply_convert_fusion.5
  911.1 7.4 bitcast_add_fusion.4
  918.5 11.2 bitcast_add_fusion.5
  933.5 8.1 fusion.183
  945.6 13.2 multiply_reduce_fusion.3
  958.8 14.9 multiply_convert_fusion.5
  973.6 8.6 bitcast_add_fusion.4
  982.3 12.4 bitcast_add_fusion.5
  999.6 14.1 convolution_convert_fusion.2
  1013.7 14.0 convolution_convert_fusion.1
  1028.5 14.7 convolution_convert_fusion
  1054.5 7.2 convolution_convert_fusion.5
  1074.7 6.6 fusion.61
  1081.4 14.2 convolution_convert_fusion.3
  1104.2 5.8 add_convert_fusion
  1112.8 62.7 %reduce-scatter.24.cloned.1.call-done = bf16[256,2048]{1,0:T(8,128)(2,1)} async-done(((bf16[2048,2048]{1,0:T(8,128)(2,1)}), bf16[256,2048]{1,0:T(8,128)(2,1)}) %reduce-scatter.24.cloned.1.call-update) | async-done | bytes 1048592 | tf_op jit(solution)/shard_map/reduce_scatter | solution.py:123
  1178.3 71.9 %reduce-scatter.26.cloned.1.call-done = bf16[2048,256]{1,0:T(8,128)(2,1)} async-done(((bf16[2048,2048]{1,0:T(8,128)(2,1)}), bf16[2048,256]{1,0:T(8,128)(2,1)}) %reduce-scatter.26.cloned.1.call-update) | async-done | bytes 1048592 | tf_op jit(solution)/shard_map/reduce_scatter | solution.py:123
  1252.9 41.6 %reduce-scatter.14.cloned.1.call-done = bf16[256,512]{1,0:T(8,128)(2,1)} async-done(((bf16[2048,512]{1,0:T(8,128)(2,1)}), bf16[256,512]{1,0:T(8,128)(2,1)}) %reduce-scatter.14.cloned.1.call-update) | async-done | bytes 262160 | tf_op jit(solution)/shard_map/reduce_scatter | solution.py:123
  1296.2 42.5 %reduce-scatter.20.cloned.1.call-done = bf16[512,256]{1,0:T(8,128)(2,1)} async-done(((bf16[512,2048]{1,0:T(8,128)(2,1)}), bf16[512,256]{1,0:T(8,128)(2,1)}) %reduce-scatter.20.cloned.1.call-update) | async-done | bytes 262160 | tf_op jit(solution)/shard_map/reduce_scatter | solution.py:123
  1340.5 42.7 %reduce-scatter.16.cloned.1.call-done = bf16[256,512]{1,0:T(8,128)(2,1)} async-done(((bf16[2048,512]{1,0:T(8,128)(2,1)}), bf16[256,512]{1,0:T(8,128)(2,1)}) %reduce-scatter.16.cloned.1.call-update) | async-done | bytes 262160 | tf_op jit(solution)/shard_map/reduce_scatter | solution.py:123
  1385.0 42.5 %reduce-scatter.18.cloned.1.call-done = bf16[256,512]{1,0:T(8,128)(2,1)} async-done(((bf16[2048,512]{1,0:T(8,128)(2,1)}), bf16[256,512]{1,0:T(8,128)(2,1)}) %reduce-scatter.18.cloned.1.call-update) | async-done | bytes 262160 | tf_op jit(solution)/shard_map/reduce_scatter | solution.py:123
  1429.3 292.3 %all-reduce.6.cloned.1.call-done = (bf16[1024,2048]{1,0:T(8,128)(2,1)}, bf16[1024,2048]{1,0:T(8,128)(2,1)}) async-done(((bf16[1024,2048]{1,0:T(8,128)(2,1)}, bf16[1024,2048]{1,0:T(8,128)(2,1)}), (bf16[1024,2048]{1,0:T(8,128)(2,1)}, bf16[1024,2048]{1,0:T(8,128)(2,1)})) %all-reduce.6.cloned.1.call-update) | async-done | bytes 8388624 | tf_op jit(solution)/shard_map/psum | solution.py:191
  1721.6 6.6 convert_reduce_fusion
  1728.2 10.5 fusion.40
  (282 shorter events, 173.3 us)
Async XLA Ops:
  7.2 33.8 %all-gather.15.cloned.1.call-start = ((), (), s32[]{:S(2)}) async-start(), calls=%async_computation.10 | async-start | bytes 2359296 | tf_op jit(solution)/shard_map/all_gather | solution.py:151
  9.0 62.2 %all-gather.19.cloned.1.call-start = ((), (), s32[]{:S(2)}) async-start(), calls=%async_computation.12 | async-start | bytes 2359296 | tf_op jit(solution)/shard_map/all_gather | solution.py:152
  10.9 90.7 %all-gather.13.cloned.1.call-start = ((), (), s32[]{:S(2)}) async-start(), calls=%async_computation.9 | async-start | bytes 2359296 | tf_op jit(solution)/shard_map/all_gather | solution.py:150
  12.7 115.8 %all-gather.17.cloned.1.call-start = ((), (), s32[]{:S(2)}) async-start(), calls=%async_computation.11 | async-start | bytes 3145728 | tf_op jit(solution)/shard_map/all_gather | solution.py:172
  14.8 31.7 %copy-start.23 = (f32[1024,128]{0,1:T(8,128)}, f32[1024,128]{0,1:T(8,128)S(1)}, u32[]{:S(2)}) copy-start(f32[1024,128]{0,1:T(8,128)S(1)} %get-tuple-element.318) | copy-start | bytes 1572868
  14.8 31.7 %copy-start.25 = (f32[1024,128]{0,1:T(8,128)}, f32[1024,128]{0,1:T(8,128)S(1)}, u32[]{:S(2)}) copy-start(f32[1024,128]{0,1:T(8,128)S(1)} %get-tuple-element.319) | copy-start | bytes 1572868
  18.0 56.2 %copy-start.38 = (f32[1024]{0:T(1024)}, f32[1024]{0:T(1024)S(1)}, u32[]{:S(2)}) copy-start(f32[1024]{0:T(1024)S(1)} %broadcast_multiply_fusion.7) | copy-start | bytes 12292
  19.3 54.9 %copy-start.42 = (f32[1024]{0:T(1024)}, f32[1024]{0:T(1024)S(1)}, u32[]{:S(2)}) copy-start(f32[1024]{0:T(1024)S(1)} %add_rsqrt_fusion.1) | copy-start | bytes 12292
  48.1 83.5 %all-gather.29.cloned.1.call-start = ((), (), s32[]{:S(2)}) async-start(), calls=%async_computation.27 | async-start | bytes 3145728 | tf_op jit(solution)/shard_map/all_gather | solution.py:173
  79.9 86.7 %all-gather.21.cloned.1.call-start = ((), (), s32[]{:S(2)}) async-start(), calls=%async_computation.13 | async-start | bytes 2359296 | tf_op jit(solution)/shard_map/all_gather | solution.py:153
  80.7 247.7 %all-reduce.4.cloned.1.call-start = ((), (), s32[]{:S(2)}) async-start(), calls=%async_computation.14 | async-start | bytes 8388608 | tf_op jit(solution)/shard_map/psum | solution.py:183
  166.6 6.3 copy-start.40
  172.9 211.2 %all-gather.23.cloned.1.call-start = ((), (), s32[]{:S(2)}) async-start(), calls=%async_computation.15 | async-start | bytes 9437184 | tf_op jit(solution)/shard_map/all_gather | solution.py:156
  175.7 265.2 %all-gather.25.cloned.1.call-start = ((), (), s32[]{:S(2)}) async-start(), calls=%async_computation.16 | async-start | bytes 9437184 | tf_op jit(solution)/shard_map/all_gather | solution.py:157
  178.5 320.6 %all-gather.27.cloned.1.call-start = ((), (), s32[]{:S(2)}) async-start(), calls=%async_computation.17 | async-start | bytes 9437184 | tf_op jit(solution)/shard_map/all_gather | solution.py:158
  181.6 653.5 %all-gather.31.cloned.1.call-start = ((), (), s32[]{:S(2)}) async-start(), calls=%async_computation.28 | async-start | bytes 20971520 | tf_op jit(solution)/shard_map/all_gather | solution.py:12
  182.3 673.5 %copy-start.44 = (f32[1024]{0:T(1024)}, f32[1024]{0:T(1024)S(1)}, u32[]{:S(2)}) copy-start(f32[1024]{0:T(1024)S(1)} %fusion.106) | copy-start | bytes 12292
  328.4 5.9 copy-start.6
  521.3 14.7 copy-start.46
  521.3 14.7 copy-start.49
  548.2 513.6 %reduce-scatter.10.cloned.1.call-start = ((), (), s32[]{:S(2)}) async-start(), calls=%async_computation.18 | async-start | bytes 6291456 | tf_op jit(solution)/shard_map/reduce_scatter | solution.py:236
  847.4 8.5 copy-start.2
  847.4 8.5 copy-start.7
  847.4 8.5 copy-start.15
  855.9 9.5 copy-start.48
  870.9 8.2 copy-start.9
  883.0 13.2 copy-start.12
  911.1 7.4 copy-start.13
  911.1 18.7 %slice-start = ((s8[8388608]{0:T(1024)(128)(4,1)}), s8[4194304]{0:T(1024)(128)(4,1)S(1)}, s32[]{:S(2)}) async-start(s8[8388608]{0:T(1024)(128)(4,1)} %bitcast.247), calls=%async_computation.30 | async-start | bytes 8388608 | tf_op jit(solution)/shard_map/while
  918.5 11.2 slice-start.1
  918.5 11.3 copy-start.16
  933.5 8.1 copy-start.9
  945.6 13.2 copy-start.12
  973.6 8.6 copy-start.13
  973.6 21.1 %slice-start = ((s8[8388608]{0:T(1024)(128)(4,1)}), s8[4194304]{0:T(1024)(128)(4,1)S(1)}, s32[]{:S(2)}) async-start(s8[8388608]{0:T(1024)(128)(4,1)} %bitcast.247), calls=%async_computation.30 | async-start | bytes 8388608 | tf_op jit(solution)/shard_map/while
  982.3 12.4 slice-start.1
  982.3 12.4 copy-start.16
  998.8 73.1 %reduce-scatter.12.cloned.1.call-start = ((), (), s32[]{:S(2)}) async-start(), calls=%async_computation.19 | async-start | bytes 6291456 | tf_op jit(solution)/shard_map/reduce_scatter | solution.py:237
  999.6 110.5 %reduce-scatter.22.cloned.1.call-start = ((), (), s32[]{:S(2)}) async-start(), calls=%async_computation.24 | async-start | bytes 9437184 | tf_op jit(solution)/shard_map/reduce_scatter | solution.py:123
  1013.7 161.8 %reduce-scatter.24.cloned.1.call-start = ((), (), s32[]{:S(2)}) async-start(), calls=%async_computation.25 | async-start | bytes 9437184 | tf_op jit(solution)/shard_map/reduce_scatter | solution.py:123
  1027.8 222.3 %reduce-scatter.26.cloned.1.call-start = ((), (), s32[]{:S(2)}) async-start(), calls=%async_computation.26 | async-start | bytes 9437184 | tf_op jit(solution)/shard_map/reduce_scatter | solution.py:123
  1043.2 251.2 %reduce-scatter.14.cloned.1.call-start = ((), (), s32[]{:S(2)}) async-start(), calls=%async_computation.20 | async-start | bytes 2359296 | tf_op jit(solution)/shard_map/reduce_scatter | solution.py:123
  1054.2 284.5 %reduce-scatter.20.cloned.1.call-start = ((), (), s32[]{:S(2)}) async-start(), calls=%async_computation.23 | async-start | bytes 2359296 | tf_op jit(solution)/shard_map/reduce_scatter | solution.py:123
  1061.8 321.4 %reduce-scatter.16.cloned.1.call-start = ((), (), s32[]{:S(2)}) async-start(), calls=%async_computation.21 | async-start | bytes 2359296 | tf_op jit(solution)/shard_map/reduce_scatter | solution.py:123
  1070.7 356.8 %reduce-scatter.18.cloned.1.call-start = ((), (), s32[]{:S(2)}) async-start(), calls=%async_computation.22 | async-start | bytes 2359296 | tf_op jit(solution)/shard_map/reduce_scatter | solution.py:123
  1081.4 640.2 %all-reduce.6.cloned.1.call-start = ((), (), s32[]{:S(2)}) async-start(), calls=%async_computation.29 | async-start | bytes 16777216 | tf_op jit(solution)/shard_map/psum | solution.py:191
  1721.6 6.7 copy-start.5
  1721.6 6.7 copy-start.8
  (36 other events, 100.1 us)
Sparse Core Ops, SparseCore 0:
  10.4 30.4 all-gather.14
  43.4 27.7 all-gather.18
  73.7 27.7 all-gather.12
  103.5 10.5 all-gather.16
  115.5 11.7 all-gather.28
  129.0 29.2 all-gather.20
  173.0 155.3 all-reduce.3
  330.8 53.2 all-gather.22
  386.6 54.2 all-gather.24
  443.2 55.8 all-gather.26
  548.3 286.7 all-gather.30
  998.9 10.0 reduce-scatter.9
  1011.3 13.1 reduce-scatter.11
  1027.9 72.7 reduce-scatter.21
  1104.0 71.4 reduce-scatter.23
  1178.8 71.2 reduce-scatter.25
  1253.3 41.1 reduce-scatter.13
  1297.6 41.1 reduce-scatter.19
  1342.0 41.1 reduce-scatter.15
  1386.3 41.1 reduce-scatter.17
  1430.6 290.8 all-reduce.5
